TPU v7x, 256 devices: a 4x2x16 block of a 4x16x16 slice. The times are simulated.
256 devices in a mesh: grp: 2 (over y), slab: 32 (over z, core), ang: 4 (over x).
Axes of the slice: x: 4, y: 2, z: 16, core: 2. Of those that a mesh axis runs over, the one named last changes fastest.
The devices are a block of a 4x16x16 slice.
Arguments:
- volume: bfloat16 [128, 256, 1024], P(('grp', 'slab')), parts along dimension 0, may hold values from -6 to 6
- ray_weights: bfloat16 [8, 1024, 1024], P('ang'), may hold values from -0.0234375 to 0.0234375
- row_offsets: int32 [8, 64], P('ang'), may hold values from 0 to 8
- measured: float32 [16, 256, 1024], P(('grp', 'ang'), 'slab'), parts along dimension 0, may hold values from -6 to 6
- shifts: float32 [16], P(('grp', 'ang')), parts along dimension 0, may hold values from -4 to 4
Outputs:
- updated_volume: bfloat16 [128, 256, 1024], P(('grp', 'slab')), parts along dimension 0
- last_residual: float32 [16, 256, 1024], P(('grp', 'ang'), 'slab'), parts along dimension 0
- shift_slope: float32 [16], P(('grp', 'ang')), parts along dimension 0
There are 2 independent parts, one for each index of `grp`. A program takes and returns all parts, laid end to end along the dimension named above; an argument that names none is the same for every part. Nothing has to cross between parts.
All inputs are finite; a program needn't handle non-finite values.
Results may differ from a plain program's by a relative error of at most 0.006.
Values may be sent and summed in bfloat16 or wider, within the bound.
No kernel may reach another device: no remote copies, remote signals or barrier semaphores. Data moves between devices by JAX's collectives and lax.ppermute only.
A program may use at most 128 MiB of HBM per device.

v0:
```python
import math
import jax
import jax.numpy as jnp
from jax import lax
from jax.sharding import Mesh
from jax.sharding import PartitionSpec as P

Y = 256
X = 1024
U = 1024
OFF = 8
ROUNDS = 2
SLAB = ("slab_0", "slab_1")
GRP_SLAB = ("grp", "slab_0", "slab_1")
step_size = 0.5


def own_block(tiles, axes, order):
    lengths = [lax.axis_size(a) for a in axes]
    tiles = tiles.reshape(*lengths, *tiles.shape[1:])
    tiles = tiles.transpose(*order, *range(len(axes), tiles.ndim))
    tiles = tiles.reshape(-1, *tiles.shape[len(axes) :])
    for k in order:
        tiles = lax.psum_scatter(tiles, axes[k], scatter_dimension=0, tiled=True)
    return tiles[0]


def in_blocks(shard, dim, length):
    lengths = shard.shape
    tiles = shard.reshape(*lengths[:dim], length, lengths[dim] // length, *lengths[dim + 1 :])
    return jnp.moveaxis(tiles, dim, 0)


def summed_rows(shard, axes, order, dim):
    length = lax.axis_size(axes)
    return own_block(in_blocks(shard, dim, length), axes, order)


def in_order(tiles, dim):
    lengths = list(tiles.shape[1:])
    lengths[dim] *= tiles.shape[0]
    return jnp.moveaxis(tiles, 0, dim).reshape(lengths)


def stacked_from(shard, axes, order):
    tiles = shard
    for k in order:
        tiles = lax.all_gather(tiles, axes[k])
    done = order[::-1]
    back = [done.index(k) for k in range(len(axes))]
    tiles = tiles.transpose(*back, *range(len(axes), tiles.ndim))
    return tiles.reshape(-1, *shard.shape)


def gather_axes(shard, axes, order, dim):
    return in_order(stacked_from(shard, axes, order), dim)


def from_everyone(shard, axis):
    copies = jnp.broadcast_to(shard, (lax.axis_size(axis), *shard.shape))
    return lax.all_to_all(copies, axis, split_axis=0, concat_axis=0, tiled=True)


def over_copies(shard, axis):
    return from_everyone(shard, axis).sum(axis=0)


def move_down(products, tilt_table):
    base = jnp.zeros((products.shape[1] + OFF, U), jnp.float32)
    placed = jax.vmap(
        lambda block, shift_rows: lax.dynamic_update_slice(base, block, (shift_rows, jnp.int32(0)))
    )(products, tilt_table)
    return jnp.sum(placed, axis=0)


def backproject(extended, tilt_table, ray_weights, band_rows):
    slices_count = tilt_table.shape[1]
    running = jnp.zeros((slices_count * band_rows, X), jnp.float32)
    for angle_index in range(ray_weights.shape[0]):
        source = extended[angle_index]
        picked = jax.vmap(
            lambda shift_rows: lax.dynamic_slice(source, (shift_rows, jnp.int32(0)), (band_rows, U))
        )(tilt_table[angle_index])
        running = running + lax.dot_general(
            picked.reshape(slices_count * band_rows, U),
            ray_weights[angle_index],
            (((1,), (1,)), ((), ())),
            preferred_element_type=jnp.float32,
        )
    return running


def apply_update(current, running):
    partial_value = lax.optimization_barrier(running.reshape(current.shape).astype(jnp.bfloat16))
    partial_wide = partial_value.astype(jnp.float32)
    gradient = lax.psum(partial_wide, "ang")
    renewed = (current.astype(jnp.float32) - step_size * gradient).astype(jnp.bfloat16)
    return renewed


def per_device(volume, ray_weights, row_offsets, measured, shifts):
    angles_here = ray_weights.shape[0]
    band_rows = measured.shape[1]
    highest = lax.Precision.HIGHEST
    numbers = lax.iota(jnp.int32, U)
    turns = numbers[:, None] * numbers[None, :] % U
    radians = turns.astype(jnp.float32) * (2.0 * math.pi / U)
    cosine = jnp.cos(radians)
    sine = jnp.sin(radians)
    signed = jnp.where(numbers <= (U - 1) // 2, numbers, numbers - U)
    omega = signed.astype(jnp.float32) * (2.0 * math.pi / U)
    flat_rows = measured.reshape(angles_here * band_rows, U)
    real_part = jnp.dot(flat_rows, cosine, precision=highest).reshape(angles_here, band_rows, U)
    imag_part = -jnp.dot(flat_rows, sine, precision=highest).reshape(angles_here, band_rows, U)
    phase = omega[None, None, :] * shifts[:, None, None]
    turned_real = real_part * jnp.cos(phase) + imag_part * jnp.sin(phase)
    turned_imag = imag_part * jnp.cos(phase) - real_part * jnp.sin(phase)
    first_half = jnp.concatenate([turned_real, omega * turned_imag], axis=0).reshape(-1, U)
    second_half = jnp.concatenate([turned_imag, -omega * turned_real], axis=0).reshape(-1, U)
    inverse = (
        jnp.dot(first_half, cosine, precision=highest)
        - jnp.dot(second_half, sine, precision=highest)
    ) / U
    inverse = inverse.reshape(2, angles_here, band_rows, U)
    shifted = inverse[0]
    slope_field = inverse[1]
    projection = shifted
    residual = shifted
    current = volume
    slices_here = volume.shape[0]
    tilt_table = lax.dynamic_slice_in_dim(
        row_offsets, lax.axis_index(SLAB) * slices_here, slices_here, 1
    )
    for round_index in range(ROUNDS):
        flattened = current.reshape(slices_here * Y, X)
        partials = jnp.stack(
            [
                move_down(
                    jnp.dot(
                        flattened, ray_weights[angle_index], preferred_element_type=jnp.float32
                    ).reshape(slices_here, Y, U),
                    tilt_table[angle_index],
                )[:Y]
                for angle_index in range(angles_here)
            ]
        )
        projection = summed_rows(partials, SLAB, (1, 0), 1)
        residual = projection - shifted
        rounded = residual.astype(jnp.bfloat16)
        gathered = gather_axes(rounded, SLAB, (0, 1), 1)
        extended = jnp.concatenate(
            [gathered, jnp.zeros((angles_here, OFF, U), jnp.bfloat16)], axis=1
        )
        running = backproject(extended, tilt_table, ray_weights, Y)
        current = apply_update(current, running)
    local_dot = jnp.sum(projection * slope_field, axis=(1, 2))
    shift_slope = over_copies(local_dot, SLAB) / math.sqrt(Y * U)
    return (current, residual, shift_slope)


def solution(mesh):
    split = Mesh(
        mesh.devices.reshape(mesh.shape["grp"], 16, 2, mesh.shape["ang"]),
        ("grp", "slab_0", "slab_1", "ang"),
    )
    placed = (
        P(GRP_SLAB, None, None),
        P("ang", None, None),
        P("ang", None),
        P(("grp", "ang"), SLAB, None),
        P(("grp", "ang")),
    )
    return jax.shard_map(
        per_device,
        mesh=split,
        in_specs=placed,
        out_specs=(P(GRP_SLAB, None, None), P(("grp", "ang"), SLAB, None), P(("grp", "ang"))),
        check_vma=False,
    )
```

profile of v0, /device:TPU:34, one launch (start us, length us, event | category | flops | bytes accessed | tf_op | source)
XLA Modules:
  0.0 536.4 jit_solution(7147799609888639398)
XLA Ops:
  7.3 4.7 fusion.16
  15.2 18.0 %while.12 = (s32[]{:T(128)}, f32[2,264,1024]{2,1,0:T(8,128)S(1)}, s32[2,3]{1,0:T(2,128)S(1)}, f32[2,256,1024]{2,1,0:T(8,128)}, s32[]{:T(128)}, /*index=5*/s32[3]{0:T(128)S(1)}, s32[]{:T(128)}) while((s32[]{:T(128)}, f32[2,264,1024]{2,1,0:T(8,128)S(1)}, s32[2,3]{1,0:T(2,128)S(1)}, f32[2,256,1024]{2,1,0:T(8,128)}, s32[]{:T(128)}, ...), condition=%wide.while_cond.4, body=%wide.while_body.4.sunk | while | flops 262163 | bytes 5243051 | solution.py:71
  34.9 24.1 %while.13 = (s32[]{:T(128)}, f32[2,264,1024]{2,1,0:T(8,128)}, s32[2,3]{1,0:T(2,128)S(1)}, f32[2,256,1024]{2,1,0:T(8,128)}, s32[]{:T(128)}, /*index=5*/s32[3]{0:T(128)S(1)}, s32[]{:T(128)}) while((s32[]{:T(128)}, f32[2,264,1024]{2,1,0:T(8,128)}, s32[2,3]{1,0:T(2,128)S(1)}, f32[2,256,1024]{2,1,0:T(8,128)}, s32[]{:T(128)}, /*index=5*/s32[3]{0:T(128)S(1)}, ...), condition=%wide.while_cond.5, body=%wide.while_body.5.sunk | while | flops 262163 | bytes 5243051 | solution.py:71
  41.9 5.1 dynamic-update-slice.33
  53.9 5.1 dynamic-update-slice.33
  63.3 32.5 %reduce-scatter.5.cloned.1.call-done = f32[16,2,8,1024]{3,2,1,0:T(8,128)} async-done(((f32[32,2,8,1024]{3,2,1,0:T(8,128)}), f32[16,2,8,1024]{3,2,1,0:T(8,128)}) %reduce-scatter.5.cloned.1.call-update) | async-done | bytes 1048592 | tf_op jit(solution)/shard_map/reduce_scatter | solution.py:24
  96.4 17.8 %fusion.50 = f32[2,8,1024]{2,1,0:T(8,128)S(1)} fusion(f32[2,8,1024]{2,1,0:T(8,128)S(1)} %copy-done), kind=kOutput, calls=%fused_computation.67 | convolution fusion | flops 216006656 | bytes 131072 | tf_op jit(solution)/shard_map/dot_general | solution.py:113
  114.3 18.0 %broadcast_multiply_fusion = (f32[2,8,1024]{2,1,0:T(8,128)S(1)}, f32[2,8,1024]{2,1,0:T(8,128)S(1)}, f32[2,8,1024]{2,1,0:T(8,128)S(1)}, f32[2,8,1024]{2,1,0:T(8,128)S(1)}) fusion(f32[1024]{0:T(1024)S(1)} %get-tuple-element.358, f32[2,1024]{1,0:T(2,128)S(1)} %get-tuple-element.348, f32[2,8,1024]{2,1,0:T(8,128)S(1)} %fusion.50, ...), kind=kOutput, calls=%fused_computation.102 | convolution fusion | flops 216154112 | bytes 417792 | tf_op jit(solution)/shard_map/dot_general | solution.py:114
  132.3 18.4 %fusion.24 = f32[32,1024]{1,0:T(8,128)S(1)} fusion(f32[2,8,1024]{2,1,0:T(8,128)S(1)} %get-tuple-element.345, f32[2,8,1024]{2,1,0:T(8,128)S(1)} %get-tuple-element.324), kind=kOutput, calls=%fused_computation.53 | convolution fusion | flops 417366016 | bytes 262144 | tf_op jit(solution)/shard_map/dot_general | solution.py:121
  150.7 18.0 %fusion.47 = f32[32,1024]{1,0:T(8,128)S(1)} fusion(f32[32,1024]{1,0:T(8,128)S(1)} %fusion.24, f32[2,8,1024]{2,1,0:T(8,128)S(1)} %get-tuple-element.323, f32[2,8,1024]{2,1,0:T(8,128)S(1)} %get-tuple-element.346), kind=kOutput, calls=%fused_computation.66 | convolution fusion | flops 417431552 | bytes 393216 | tf_op jit(solution)/shard_map/dot_general | solution.py:122
  170.0 34.9 %all_gather.20 = bf16[16,2,8,1024]{3,2,1,0:T(8,128)(2,1)} all-gather(bf16[1,2,8,1024]{3,2,1,0:T(8,128)(2,1)S(1)} %fusion.69), channel_id=1, replica_groups=mesh['grp'=2,'slab_0'=16,'slab_1'=2,'ang'=4] {'slab_0'}, dimensions={0}, use_global_device_ids=true | all-gather | bytes 557056 | tf_op jit(solution)/shard_map/all_gather | solution.py:48
  205.3 15.5 %all-gather.5.cloned.1.call-done = bf16[32,2,8,1024]{3,2,1,0:T(8,128)(2,1)} async-done(((bf16[16,2,8,1024]{3,2,1,0:T(8,128)(2,1)}), bf16[32,2,8,1024]{3,2,1,0:T(8,128)(2,1)}) %all-gather.5.cloned.1.call-update) | async-done | bytes 1048592 | tf_op jit(solution)/shard_map/all_gather | solution.py:48
  223.0 4.2 fusion.10
  231.3 42.2 %all-reduce.6 = f32[2,256,1024]{2,1,0:T(8,128)S(1)} all-reduce(bf16[2,256,1024]{2,1,0:T(8,128)(2,1)S(1)} %bitcast.233), channel_id=1, replica_groups=mesh['grp'=2,'slab_0'=16,'slab_1'=2,'ang'=4] {'ang'}, use_global_device_ids=true, to_apply=%region_6.7 | all-reduce | flops 524288 | bytes 3145728 | tf_op jit(solution)/shard_map/psum | solution.py:96
  281.5 17.7 %while.14 = (s32[]{:T(128)}, f32[2,264,1024]{2,1,0:T(8,128)S(1)}, s32[2,3]{1,0:T(2,128)S(1)}, f32[2,256,1024]{2,1,0:T(8,128)}, s32[]{:T(128)}, /*index=5*/s32[3]{0:T(128)S(1)}, s32[]{:T(128)}) while((s32[]{:T(128)}, f32[2,264,1024]{2,1,0:T(8,128)S(1)}, s32[2,3]{1,0:T(2,128)S(1)}, f32[2,256,1024]{2,1,0:T(8,128)}, s32[]{:T(128)}, ...), condition=%wide.while_cond.6, body=%wide.while_body.6.sunk | while | flops 262163 | bytes 5243051 | solution.py:71
  300.7 18.1 %while.15 = (s32[]{:T(128)}, f32[2,264,1024]{2,1,0:T(8,128)S(1)}, s32[2,3]{1,0:T(2,128)S(1)}, f32[2,256,1024]{2,1,0:T(8,128)}, s32[]{:T(128)}, /*index=5*/s32[3]{0:T(128)S(1)}, s32[]{:T(128)}) while((s32[]{:T(128)}, f32[2,264,1024]{2,1,0:T(8,128)S(1)}, s32[2,3]{1,0:T(2,128)S(1)}, f32[2,256,1024]{2,1,0:T(8,128)}, s32[]{:T(128)}, ...), condition=%wide.while_cond.7, body=%wide.while_body.7.sunk | while | flops 262163 | bytes 5243051 | solution.py:71
  322.2 20.0 %reduce-scatter.9.cloned.1.call-done = f32[16,2,8,1024]{3,2,1,0:T(8,128)} async-done(((f32[32,2,8,1024]{3,2,1,0:T(8,128)}), f32[16,2,8,1024]{3,2,1,0:T(8,128)}) %reduce-scatter.9.cloned.1.call-update) | async-done | bytes 1048592 | tf_op jit(solution)/shard_map/reduce_scatter | solution.py:24
  342.3 73.3 %reduce-scatter.11.cloned.1.call-done = f32[1,2,8,1024]{3,2,1,0:T(8,128)} async-done(((f32[16,2,8,1024]{3,2,1,0:T(8,128)}), f32[1,2,8,1024]{3,2,1,0:T(8,128)}) %reduce-scatter.11.cloned.1.call-update) | async-done | bytes 65552 | tf_op jit(solution)/shard_map/reduce_scatter | solution.py:24
  416.4 32.8 %all_gather.23 = bf16[16,2,8,1024]{3,2,1,0:T(8,128)(2,1)} all-gather(bf16[1,2,8,1024]{3,2,1,0:T(8,128)(2,1)S(1)} %fusion.70), channel_id=1, replica_groups=mesh['grp'=2,'slab_0'=16,'slab_1'=2,'ang'=4] {'slab_0'}, dimensions={0}, use_global_device_ids=true | all-gather | bytes 557056 | tf_op jit(solution)/shard_map/all_gather | solution.py:48
  451.4 10.5 %all-to-all-start = ((f32[32,1,2]{2,1,0:T(1,128)}), f32[32,1,2]{2,1,0:T(1,128)S(1)}, u32[]{:S(2)}, u32[]{:S(2)}) async-start(f32[32,1,2]{2,1,0:T(1,128)} %broadcast_in_dim.7), calls=%async_computation.4 | async-start | bytes 32768 | tf_op jit(solution)/shard_map/all_to_all | solution.py:61
  461.9 12.1 %all-to-all-done = f32[32,1,2]{2,1,0:T(1,128)S(1)} async-done(((f32[32,1,2]{2,1,0:T(1,128)}), f32[32,1,2]{2,1,0:T(1,128)S(1)}, u32[]{:S(2)}, u32[]{:S(2)}) %all-to-all-start) | async-done | bytes 288 | tf_op jit(solution)/shard_map/all_to_all | solution.py:61
  476.7 4.2 fusion.12
  481.5 4.5 add_convert_fusion
  486.0 42.0 %all-reduce.7 = f32[2,256,1024]{2,1,0:T(8,128)S(1)} all-reduce(bf16[2,256,1024]{2,1,0:T(8,128)(2,1)} %bitcast.234), channel_id=1, replica_groups=mesh['grp'=2,'slab_0'=16,'slab_1'=2,'ang'=4] {'ang'}, use_global_device_ids=true, to_apply=%region_13.14 | all-reduce | flops 524288 | bytes 3145728 | tf_op jit(solution)/shard_map/psum | solution.py:96
  (146 shorter events, 107.0 us)
Async XLA Ops:
  7.2 89.2 %copy-start = (f32[2,8,1024]{2,1,0:T(8,128)S(1)}, f32[2,8,1024]{2,1,0:T(8,128)}, u32[]{:S(2)}) copy-start(f32[2,8,1024]{2,1,0:T(8,128)} %param.8) | copy-start | bytes 196612
  7.2 88.6 %reduce-scatter.5.cloned.1.call-start = ((), (), s32[]{:S(2)}) async-start(), calls=%async_computation.5 | async-start | bytes 3145728 | tf_op jit(solution)/shard_map/reduce_scatter | solution.py:24
  7.3 4.7 copy-start.5
  7.3 4.7 copy-start.10
  12.0 2.6 copy-start.7
  12.0 2.7 copy-start.8
  14.6 0.7 copy-start.6
  63.1 33.1 %copy-start.9 = (f32[2]{0:T(128)S(1)}, f32[2]{0:T(128)}, u32[]{:S(2)}) copy-start(f32[2]{0:T(128)} %param.9) | copy-start | bytes 28
  63.2 106.0 %reduce-scatter.7.cloned.1.call-start = ((), (), s32[]{:S(2)}) async-start(), calls=%async_computation.6 | async-start | bytes 1114112 | tf_op jit(solution)/shard_map/reduce_scatter | solution.py:24
  95.8 124.9 %all-gather.5.cloned.1.call-start = ((), (), s32[]{:S(2)}) async-start(), calls=%async_computation.9 | async-start | bytes 1572864 | tf_op jit(solution)/shard_map/all_gather | solution.py:48
  205.0 137.2 %reduce-scatter.9.cloned.1.call-start = ((), (), s32[]{:S(2)}) async-start(), calls=%async_computation.7 | async-start | bytes 3145728 | tf_op jit(solution)/shard_map/reduce_scatter | solution.py:24
  273.5 2.5 copy-start.11
  276.0 2.6 copy-start.3
  319.0 1.2 copy-start.2
  322.1 93.5 %reduce-scatter.11.cloned.1.call-start = ((), (), s32[]{:S(2)}) async-start(), calls=%async_computation.8 | async-start | bytes 1114112 | tf_op jit(solution)/shard_map/reduce_scatter | solution.py:24
  342.3 132.4 %all-gather.7.cloned.1.call-start = ((), (), s32[]{:S(2)}) async-start(), calls=%async_computation.10 | async-start | bytes 1572864 | tf_op jit(solution)/shard_map/all_gather | solution.py:48
  451.4 22.6 %all-to-all-start = ((f32[32,1,2]{2,1,0:T(1,128)}), f32[32,1,2]{2,1,0:T(1,128)S(1)}, u32[]{:S(2)}, u32[]{:S(2)}) async-start(f32[32,1,2]{2,1,0:T(1,128)} %broadcast_in_dim.7), calls=%async_computation.4 | async-start | bytes 32768 | tf_op jit(solution)/shard_map/all_to_all | solution.py:61
  486.0 42.0 %copy-start.4 = (bf16[2,256,1024]{2,1,0:T(8,128)(2,1)S(1)}, bf16[2,256,1024]{2,1,0:T(8,128)(2,1)}, u32[]{:S(2)}) copy-start(bf16[2,256,1024]{2,1,0:T(8,128)(2,1)} %copy-done.3) | copy-start | bytes 3145732
  486.0 43.4 %copy-start.1 = (f32[2,8,1024]{2,1,0:T(8,128)S(1)}, f32[2,8,1024]{2,1,0:T(8,128)}, u32[]{:S(2)}) copy-start(f32[2,8,1024]{2,1,0:T(8,128)} %param.8) | copy-start | bytes 196612
Sparse Core Ops, SparseCore 0:
  63.3 32.4 reduce-scatter.4
  98.3 70.8 reduce-scatter.6
  205.1 15.5 all-gather.4
  322.2 19.9 reduce-scatter.8
  344.6 70.9 reduce-scatter.10
  449.5 16.1 all-gather.6
where the time goes:
time: 542 us; the launch traced here: 536 us
  waiting for transfers between devices  154 us (28%)
  blocking collectives  152 us (28%)
  matrix products  101 us (19%)
  other arithmetic  59.6 us (11%)
  local copies, waits for them, and re-layouts  43 us (8%)
  between operations  14.8 us (3%)
  starting transfers between devices  11.1 us (2%)
    reduce_scatter x4, waiting for transfers between devices, own_block(): tiles = lax.psum_scatter(tiles, axes[k], scatter_dimension=0, tiled=True)  126 us
    psum x2, blocking collectives, apply_update(): gradient = lax.psum(partial_wide, 'ang')  84.2 us
    all_gather x2, blocking collectives, stacked_from(): tiles = lax.all_gather(tiles, axes[k])  67.7 us
    scatter x16, other arithmetic  49.3 us
    scatter x24, local copies, waits for them, and re-layouts  28.3 us
    dot_general x1, matrix products, per_device(): jnp.dot(first_half, cosine, precision=highest)  18.4 us
    dot_general x1, matrix products, per_device(): jnp.dot(flat_rows, sine, precision=highest)  18 us
    dot_general x1, matrix products, per_device(): jnp.dot(second_half, sine, precision=highest)  18 us
  transfers between devices with their start and end apart: 7, of which 6 were waited for; matrix products, arithmetic and copies ran while one was open for 14% of the time, Pallas kernels for 0%

commit v1 on v0

--- a/solution.py
+++ b/solution.py
@@ -13,6 +13,11 @@
 SLAB = ("slab_0", "slab_1")
 GRP_SLAB = ("grp", "slab_0", "slab_1")
 step_size = 0.5
+
+
+def summed_here(x, axis):
+    pieces = lax.all_gather(x, axis)
+    return jnp.sum(pieces, axis=0)
 
 
 def own_block(tiles, axes, order):
@@ -93,7 +98,7 @@
 def apply_update(current, running):
     partial_value = lax.optimization_barrier(running.reshape(current.shape).astype(jnp.bfloat16))
     partial_wide = partial_value.astype(jnp.float32)
-    gradient = lax.psum(partial_wide, "ang")
+    gradient = summed_here(partial_wide, "ang")
     renewed = (current.astype(jnp.float32) - step_size * gradient).astype(jnp.bfloat16)
     return renewed
 

time: 542 us -> 639 us (1.18)
  waiting for transfers between devices: 154 us -> 313 us
  blocking collectives: 152 us -> 92.6 us
  starting transfers between devices: 11.1 us -> 0.8 us
  other arithmetic: 59.6 us -> 67.7 us
    all_gather x0 -> x2, waiting for transfers between devices: none -> 155 us  [summed_here(): pieces = lax.all_gather(x, axis)]
    psum x2 -> x0, blocking collectives: 84.2 us -> none  [apply_update(): gradient = lax.psum(partial_wide, 'ang')]
    all_to_all x0 -> x1, blocking collectives: none -> 24.7 us  [from_everyone(): return lax.all_to_all(copies, axis, split_axis=0, concat_axis=0, tiled=True)]
    all_gather x2, waiting for transfers between devices: 15.5 us -> 31.9 us  [stacked_from(): tiles = lax.all_gather(tiles, axes[k])]
    all_to_all x1 -> x0, waiting for transfers between devices: 12.1 us -> none  [from_everyone(): return lax.all_to_all(copies, axis, split_axis=0, concat_axis=0, tiled=True)]
    all_to_all x1 -> x0, starting transfers between devices: 10.5 us -> none  [from_everyone(): return lax.all_to_all(copies, axis, split_axis=0, concat_axis=0, tiled=True)]
    reduce_sum x0 -> x2, other arithmetic: none -> 9.27 us  [summed_here(): return jnp.sum(pieces, axis=0)]
  transfers between devices with their start and end apart: 7 -> 8, of which waited for: 6 -> 8; matrix products, arithmetic and copies ran while one was open for 14% -> 12% of each run, Pallas kernels for 0% -> 0%
where the time goes in v1:
time: 639 us; the launch traced here: 633 us
  waiting for transfers between devices  313 us (49%)
  matrix products  100 us (16%)
  blocking collectives  92.6 us (14%)
  other arithmetic  67.7 us (11%)
  local copies, waits for them, and re-layouts  42.6 us (7%)
  between operations  14.8 us (2%)
    all_gather x2, waiting for transfers between devices, summed_here(): pieces = lax.all_gather(x, axis)  155 us
    reduce_scatter x4, waiting for transfers between devices, own_block(): tiles = lax.psum_scatter(tiles, axes[k], scatter_dimension=0, tiled=True)  126 us
    all_gather x2, blocking collectives, stacked_from(): tiles = lax.all_gather(tiles, axes[k])  67.9 us
    scatter x16, other arithmetic  47.1 us
    all_gather x2, waiting for transfers between devices, stacked_from(): tiles = lax.all_gather(tiles, axes[k])  31.9 us
    scatter x24, local copies, waits for them, and re-layouts  27.4 us
    all_to_all x1, blocking collectives, from_everyone(): return lax.all_to_all(copies, axis, split_axis=0, concat_axis=0, tiled=True)  24.7 us
    dot_general x1, matrix products, per_device(): jnp.dot(first_half, cosine, precision=highest)  18.4 us
  transfers between devices with their start and end apart: 8, of which 8 were waited for; matrix products, arithmetic and copies ran while one was open for 12% of the time, Pallas kernels for 0%

profile of v1, /device:TPU:34, one launch (start us, length us, event | category | flops | bytes accessed | tf_op | source)
XLA Modules:
  0.0 632.9 jit_solution(16713878553001837276)
XLA Ops:
  7.3 4.6 fusion.16
  15.2 16.5 %while.12 = (s32[]{:T(128)}, f32[2,264,1024]{2,1,0:T(8,128)S(1)}, s32[2,3]{1,0:T(2,128)S(1)}, f32[2,256,1024]{2,1,0:T(8,128)}, s32[]{:T(128)}, /*index=5*/s32[3]{0:T(128)S(1)}, s32[]{:T(128)}) while((s32[]{:T(128)}, f32[2,264,1024]{2,1,0:T(8,128)S(1)}, s32[2,3]{1,0:T(2,128)S(1)}, f32[2,256,1024]{2,1,0:T(8,128)}, s32[]{:T(128)}, ...), condition=%wide.while_cond.4, body=%wide.while_body.4.sunk | while | flops 262163 | bytes 5243051 | solution.py:76
  33.4 24.2 %while.13 = (s32[]{:T(128)}, f32[2,264,1024]{2,1,0:T(8,128)}, s32[2,3]{1,0:T(2,128)S(1)}, f32[2,256,1024]{2,1,0:T(8,128)}, s32[]{:T(128)}, /*index=5*/s32[3]{0:T(128)S(1)}, s32[]{:T(128)}) while((s32[]{:T(128)}, f32[2,264,1024]{2,1,0:T(8,128)}, s32[2,3]{1,0:T(2,128)S(1)}, f32[2,256,1024]{2,1,0:T(8,128)}, s32[]{:T(128)}, /*index=5*/s32[3]{0:T(128)S(1)}, ...), condition=%wide.while_cond.5, body=%wide.while_body.5.sunk | while | flops 262163 | bytes 5243051 | solution.py:76
  40.4 5.1 dynamic-update-slice.33
  52.5 5.1 dynamic-update-slice.33
  61.8 32.5 %reduce-scatter.5.cloned.1.call-done = f32[16,2,8,1024]{3,2,1,0:T(8,128)} async-done(((f32[32,2,8,1024]{3,2,1,0:T(8,128)}), f32[16,2,8,1024]{3,2,1,0:T(8,128)}) %reduce-scatter.5.cloned.1.call-update) | async-done | bytes 1048592 | tf_op jit(solution)/shard_map/reduce_scatter | solution.py:29
  95.0 17.8 %fusion.50 = f32[2,8,1024]{2,1,0:T(8,128)S(1)} fusion(f32[2,8,1024]{2,1,0:T(8,128)S(1)} %copy-done), kind=kOutput, calls=%fused_computation.67 | convolution fusion | flops 216006656 | bytes 131072 | tf_op jit(solution)/shard_map/dot_general | solution.py:118
  112.8 18.0 %broadcast_multiply_fusion = (f32[2,8,1024]{2,1,0:T(8,128)S(1)}, f32[2,8,1024]{2,1,0:T(8,128)S(1)}, f32[2,8,1024]{2,1,0:T(8,128)S(1)}, f32[2,8,1024]{2,1,0:T(8,128)S(1)}) fusion(f32[1024]{0:T(1024)S(1)} %get-tuple-element.358, f32[2,1024]{1,0:T(2,128)S(1)} %get-tuple-element.348, f32[2,8,1024]{2,1,0:T(8,128)S(1)} %fusion.50, ...), kind=kOutput, calls=%fused_computation.102 | convolution fusion | flops 216154112 | bytes 417792 | tf_op jit(solution)/shard_map/dot_general | solution.py:119
  130.8 18.4 %fusion.24 = f32[32,1024]{1,0:T(8,128)S(1)} fusion(f32[2,8,1024]{2,1,0:T(8,128)S(1)} %get-tuple-element.345, f32[2,8,1024]{2,1,0:T(8,128)S(1)} %get-tuple-element.324), kind=kOutput, calls=%fused_computation.53 | convolution fusion | flops 417366016 | bytes 262144 | tf_op jit(solution)/shard_map/dot_general | solution.py:126
  149.3 18.0 %fusion.47 = f32[32,1024]{1,0:T(8,128)S(1)} fusion(f32[32,1024]{1,0:T(8,128)S(1)} %fusion.24, f32[2,8,1024]{2,1,0:T(8,128)S(1)} %get-tuple-element.323, f32[2,8,1024]{2,1,0:T(8,128)S(1)} %get-tuple-element.346), kind=kOutput, calls=%fused_computation.66 | convolution fusion | flops 417431552 | bytes 393216 | tf_op jit(solution)/shard_map/dot_general | solution.py:127
  168.6 34.9 %all_gather.38 = bf16[16,2,8,1024]{3,2,1,0:T(8,128)(2,1)} all-gather(bf16[1,2,8,1024]{3,2,1,0:T(8,128)(2,1)S(1)} %fusion.69), channel_id=1, replica_groups=mesh['grp'=2,'slab_0'=16,'slab_1'=2,'ang'=4] {'slab_0'}, dimensions={0}, use_global_device_ids=true | all-gather | bytes 557056 | tf_op jit(solution)/shard_map/all_gather | solution.py:53
  203.8 15.5 %all-gather.9.cloned.1.call-done = bf16[32,2,8,1024]{3,2,1,0:T(8,128)(2,1)} async-done(((bf16[16,2,8,1024]{3,2,1,0:T(8,128)(2,1)}), bf16[32,2,8,1024]{3,2,1,0:T(8,128)(2,1)}) %all-gather.9.cloned.1.call-update) | async-done | bytes 1048592 | tf_op jit(solution)/shard_map/all_gather | solution.py:53
  231.6 90.5 %all-gather.11.cloned.1.call-done = f32[8,256,1024]{2,1,0:T(8,128)} async-done(((f32[2,256,1024]{2,1,0:T(8,128)}), f32[8,256,1024]{2,1,0:T(8,128)}) %all-gather.11.cloned.1.call-update) | async-done | bytes 8388624 | tf_op jit(solution)/shard_map/all_gather | solution.py:19
  322.1 4.6 reduce_sum.74
  334.4 17.6 %while.14 = (s32[]{:T(128)}, f32[2,264,1024]{2,1,0:T(8,128)S(1)}, s32[2,3]{1,0:T(2,128)S(1)}, f32[2,256,1024]{2,1,0:T(8,128)}, s32[]{:T(128)}, /*index=5*/s32[3]{0:T(128)S(1)}, s32[]{:T(128)}) while((s32[]{:T(128)}, f32[2,264,1024]{2,1,0:T(8,128)S(1)}, s32[2,3]{1,0:T(2,128)S(1)}, f32[2,256,1024]{2,1,0:T(8,128)}, s32[]{:T(128)}, ...), condition=%wide.while_cond.6, body=%wide.while_body.6.sunk | while | flops 262163 | bytes 5243051 | solution.py:76
  353.6 16.5 %while.15 = (s32[]{:T(128)}, f32[2,264,1024]{2,1,0:T(8,128)S(1)}, s32[2,3]{1,0:T(2,128)S(1)}, f32[2,256,1024]{2,1,0:T(8,128)}, s32[]{:T(128)}, /*index=5*/s32[3]{0:T(128)S(1)}, s32[]{:T(128)}) while((s32[]{:T(128)}, f32[2,264,1024]{2,1,0:T(8,128)S(1)}, s32[2,3]{1,0:T(2,128)S(1)}, f32[2,256,1024]{2,1,0:T(8,128)}, s32[]{:T(128)}, ...), condition=%wide.while_cond.7, body=%wide.while_body.7.sunk | while | flops 262163 | bytes 5243051 | solution.py:76
  373.4 19.8 %reduce-scatter.9.cloned.1.call-done = f32[16,2,8,1024]{3,2,1,0:T(8,128)} async-done(((f32[32,2,8,1024]{3,2,1,0:T(8,128)}), f32[16,2,8,1024]{3,2,1,0:T(8,128)}) %reduce-scatter.9.cloned.1.call-update) | async-done | bytes 1048592 | tf_op jit(solution)/shard_map/reduce_scatter | solution.py:29
  393.4 73.2 %reduce-scatter.11.cloned.1.call-done = f32[1,2,8,1024]{3,2,1,0:T(8,128)} async-done(((f32[16,2,8,1024]{3,2,1,0:T(8,128)}), f32[1,2,8,1024]{3,2,1,0:T(8,128)}) %reduce-scatter.11.cloned.1.call-update) | async-done | bytes 65552 | tf_op jit(solution)/shard_map/reduce_scatter | solution.py:29
  467.5 33.0 %all_gather.44 = bf16[16,2,8,1024]{3,2,1,0:T(8,128)(2,1)} all-gather(bf16[1,2,8,1024]{3,2,1,0:T(8,128)(2,1)S(1)} %fusion.70), channel_id=1, replica_groups=mesh['grp'=2,'slab_0'=16,'slab_1'=2,'ang'=4] {'slab_0'}, dimensions={0}, use_global_device_ids=true | all-gather | bytes 557056 | tf_op jit(solution)/shard_map/all_gather | solution.py:53
  500.6 16.4 %all-gather.13.cloned.1.call-done = bf16[32,2,8,1024]{3,2,1,0:T(8,128)(2,1)} async-done(((bf16[16,2,8,1024]{3,2,1,0:T(8,128)(2,1)}), bf16[32,2,8,1024]{3,2,1,0:T(8,128)(2,1)}) %all-gather.13.cloned.1.call-update) | async-done | bytes 1048592 | tf_op jit(solution)/shard_map/all_gather | solution.py:53
  519.2 4.2 fusion.12
  529.9 24.7 %all_to_all.6 = f32[32,1,2]{2,1,0:T(1,128)S(1)} all-to-all(f32[32,1,2]{2,1,0:T(1,128)S(1)} %broadcast_in_dim.7), channel_id=1, replica_groups=mesh['grp'=2,'slab_0'=16,'slab_1'=2,'ang'=4] {'slab_0','slab_1'}, dimensions={0} | all-to-all | bytes 512 | tf_op jit(solution)/shard_map/all_to_all | solution.py:66
  555.2 64.6 %all-gather.15.cloned.1.call-done = f32[8,256,1024]{2,1,0:T(8,128)} async-done(((f32[2,256,1024]{2,1,0:T(8,128)}), f32[8,256,1024]{2,1,0:T(8,128)}) %all-gather.15.cloned.1.call-update) | async-done | bytes 8388624 | tf_op jit(solution)/shard_map/all_gather | solution.py:19
  619.8 4.6 reduce_sum.77
  (157 shorter events, 113.6 us)
Async XLA Ops:
  7.2 87.8 %copy-start = (f32[2,8,1024]{2,1,0:T(8,128)S(1)}, f32[2,8,1024]{2,1,0:T(8,128)}, u32[]{:S(2)}) copy-start(f32[2,8,1024]{2,1,0:T(8,128)} %param.8) | copy-start | bytes 196612
  7.2 87.1 %reduce-scatter.5.cloned.1.call-start = ((), (), s32[]{:S(2)}) async-start(), calls=%async_computation.5 | async-start | bytes 3145728 | tf_op jit(solution)/shard_map/reduce_scatter | solution.py:29
  7.3 4.7 copy-start.5
  7.3 4.7 copy-start.12
  11.9 2.6 copy-start.9
  11.9 2.7 copy-start.10
  14.6 0.7 copy-start.8
  61.7 33.1 %copy-start.11 = (f32[2]{0:T(128)S(1)}, f32[2]{0:T(128)}, u32[]{:S(2)}) copy-start(f32[2]{0:T(128)} %param.9) | copy-start | bytes 28
  61.7 106.0 %reduce-scatter.7.cloned.1.call-start = ((), (), s32[]{:S(2)}) async-start(), calls=%async_computation.6 | async-start | bytes 1114112 | tf_op jit(solution)/shard_map/reduce_scatter | solution.py:29
  94.4 124.9 %all-gather.9.cloned.1.call-start = ((), (), s32[]{:S(2)}) async-start(), calls=%async_computation.9 | async-start | bytes 1572864 | tf_op jit(solution)/shard_map/all_gather | solution.py:53
  203.5 118.6 %all-gather.11.cloned.1.call-start = ((), (), s32[]{:S(2)}) async-start(), calls=%async_computation.10 | async-start | bytes 10485760 | tf_op jit(solution)/shard_map/all_gather | solution.py:19
  231.5 161.7 %reduce-scatter.9.cloned.1.call-start = ((), (), s32[]{:S(2)}) async-start(), calls=%async_computation.7 | async-start | bytes 3145728 | tf_op jit(solution)/shard_map/reduce_scatter | solution.py:29
  322.1 4.6 copy-start.6
  326.7 2.2 copy-start.13
  328.9 2.6 copy-start.3
  370.3 1.2 copy-start.2
  373.3 93.3 %reduce-scatter.11.cloned.1.call-start = ((), (), s32[]{:S(2)}) async-start(), calls=%async_computation.8 | async-start | bytes 1114112 | tf_op jit(solution)/shard_map/reduce_scatter | solution.py:29
  393.3 123.7 %all-gather.13.cloned.1.call-start = ((), (), s32[]{:S(2)}) async-start(), calls=%async_computation.11 | async-start | bytes 1572864 | tf_op jit(solution)/shard_map/all_gather | solution.py:53
  500.5 119.3 %all-gather.15.cloned.1.call-start = ((), (), s32[]{:S(2)}) async-start(), calls=%async_computation.12 | async-start | bytes 10485760 | tf_op jit(solution)/shard_map/all_gather | solution.py:19
  527.5 1.7 copy-start.7
  619.8 4.6 copy-start.4
  619.8 6.0 copy-start.1
Sparse Core Ops, SparseCore 0:
  61.9 32.4 reduce-scatter.4
  96.8 70.8 reduce-scatter.6
  203.6 15.6 all-gather.8
  231.6 90.4 all-gather.10
  373.5 19.7 reduce-scatter.8
  395.6 70.9 reduce-scatter.10
  500.6 16.2 all-gather.12
  529.3 90.4 all-gather.14
